TPU v7x, 64 devices: a 2x2x8 block of a 4x4x8 slice. The times are simulated.
64 devices in a mesh: dp: 4 (over x, y), tp: 16 (over z, core).
Axes of the slice: x: 2, y: 2, z: 8, core: 2. Of those that a mesh axis runs over, the one named last changes fastest.
The devices are a block of a 4x4x8 slice.
Arguments:
- query: bfloat16 [32, 32, 128], P('dp', 'tp'), parts along dimension 0
- k_cache: bfloat16 [32, 2048, 16, 128], P('dp', None, 'tp'), parts along dimension 0
- v_cache: bfloat16 [32, 2048, 16, 128], P('dp', None, 'tp'), parts along dimension 0
- k_new: bfloat16 [32, 16, 128], P('dp', 'tp'), parts along dimension 0
- v_new: bfloat16 [32, 16, 128], P('dp', 'tp'), parts along dimension 0
- lens: int32 [32], P('dp'), parts along dimension 0
Outputs:
- output 1: bfloat16 [32, 32, 128], P('dp', 'tp'), parts along dimension 0
- output 2: bfloat16 [32, 2048, 16, 128], P('dp', 'tp'), parts along dimension 0
- output 3: bfloat16 [32, 2048, 16, 128], P('dp', 'tp'), parts along dimension 0
There are 4 independent parts. A program takes and returns all parts, laid end to end along the dimension named above; each array names one.
All inputs are finite; a program needn't handle non-finite values.
Results may differ from a plain program's by a relative error of at most 0.00785484.
Values are sent between devices in bfloat16 or wider.
A program may use at most 768 MiB of HBM per device.

v0:
```python
import jax
import jax.numpy as jnp
from jax import lax
from jax.sharding import PartitionSpec as P

MASK_VALUE = -1e30


def solution(mesh):
    def local_step(query, k_cache, v_cache, k_new, v_new, lens):
        batch, seq_len, head_dim = k_cache.shape[0], k_cache.shape[1], k_cache.shape[3]
        positions = lax.broadcasted_iota(jnp.int32, (1, seq_len, 1, 1), 1)
        new_slot = positions == lens[:, None, None, None]
        k_upd = jnp.where(new_slot, k_new[:, None], k_cache)
        v_upd = jnp.where(new_slot, v_new[:, None], v_cache)
        k_seq = lax.all_to_all(k_upd, "tp", 1, 2, tiled=True)
        v_seq = lax.all_to_all(v_upd, "tp", 1, 2, tiled=True)
        q_all = lax.all_gather(query, "tp", axis=1, tiled=True)
        seq_local, kv_heads = k_seq.shape[1], k_seq.shape[2]
        q_heads = q_all.shape[1]
        q_grp = q_all.reshape(batch, kv_heads, q_heads // kv_heads, head_dim)
        scores = jnp.einsum("bhgd,bthd->bhgt", q_grp, k_seq, preferred_element_type=jnp.float32) * (head_dim ** -0.5)
        tok_pos = lax.axis_index("tp") * seq_local + lax.broadcasted_iota(jnp.int32, (1, 1, 1, seq_local), 3)
        valid = tok_pos <= lens[:, None, None, None]
        scores = jnp.where(valid, scores, MASK_VALUE)
        part_max = jnp.max(scores, axis=-1)
        weights = jnp.where(valid, jnp.exp(scores - part_max[..., None]), 0.0)
        part_sum = jnp.sum(weights, axis=-1)
        part_out = jnp.einsum("bhgt,bthd->bhgd", weights.astype(jnp.bfloat16), v_seq, preferred_element_type=jnp.float32)
        glob_max = lax.pmax(part_max, "tp")
        factor = jnp.exp(part_max - glob_max)
        stacked = jnp.concatenate([part_out * factor[..., None], (part_sum * factor)[..., None]], axis=-1)
        stacked = stacked.reshape(batch, q_heads, head_dim + 1)
        own_heads = lax.psum_scatter(stacked, "tp", scatter_dimension=1, tiled=True)
        attn_out = (own_heads[..., :head_dim] / own_heads[..., head_dim:]).astype(jnp.bfloat16)
        return attn_out, k_seq, v_seq

    head_spec = P("dp", "tp")
    entry_spec = P("dp", None, "tp")
    return jax.shard_map(local_step, mesh=mesh, in_specs=(head_spec, entry_spec, entry_spec, head_spec, head_spec, P("dp")), out_specs=(head_spec, P("dp", "tp"), P("dp", "tp")), check_vma=False)
```

profile of v0, /device:TPU:22, one launch (start us, length us, event | category | flops | bytes accessed | tf_op | source)
XLA Modules:
  0.0 361.3 jit_solution(7846045680686118876)
XLA Ops:
  7.2 0.8 iota_compare_fusion
  8.0 18.2 %copy_select_fusion = (bf16[8,2048,1,128]{3,0,2,1:T(8,128)(2,1)}, bf16[8,2048,1,128]{3,0,2,1:T(8,128)(2,1)S(1)}) fusion(bf16[8,2048,1,128]{3,1,2,0:T(8,128)(2,1)} %param.8, pred[8,2048]{0,1:T(8,128)(4,1)S(1)} %iota_compare_fusion, bf16[8,128]{1,0:T(8,128)(2,1)} %bitcast.28, bf16[8,2048,1,128]{3,1,2,0:T(8,128)(2,1)} %param.7, bf16[8,128]{1,0:T(8,128)(2,1)} %bitcast.29), kind=kLoop, calls=%fused_computation | loop fusion | flops 4194304 | bytes 16797696 | tf_op jit(solution)/shard_map/jit(_where)/select_n | solution.py:15
  26.2 104.8 %all_to_all.36 = bf16[8,2048,1,128]{3,0,2,1:T(8,128)(2,1)} all-to-all(bf16[8,2048,1,128]{3,0,2,1:T(8,128)(2,1)S(1)} %get-tuple-element.21), channel_id=1, replica_groups=mesh['dp'=4,'tp'=16] {'tp'}, dimensions={1} | all-to-all | bytes 8388608 | tf_op jit(solution)/shard_map/all_to_all | solution.py:16
  131.0 5.1 %all-to-all-start.1 = ((bf16[8,2048,1,128]{3,0,2,1:T(8,128)(2,1)}), bf16[8,2048,1,128]{3,0,2,1:T(8,128)(2,1)}, u32[]{:S(2)}, u32[]{:S(2)}) async-start(bf16[8,2048,1,128]{3,0,2,1:T(8,128)(2,1)} %get-tuple-element.20), calls=%async_computation.1 | async-start | bytes 8388608 | tf_op jit(solution)/shard_map/all_to_all | solution.py:17
  136.1 0.1 reduce-scatter.2.cloned.1.call-start
  136.2 105.9 %all_gather.3 = bf16[8,32,128]{2,0,1:T(8,128)(2,1)S(1)} all-gather(bf16[8,2,128]{2,0,1:T(8,128)(2,1)S(1)} %copy.46), channel_id=1, replica_groups=mesh['dp'=4,'tp'=16] {'tp'}, dimensions={1}, use_global_device_ids=true | all-gather | bytes 69632 | tf_op jit(solution)/shard_map/all_gather | solution.py:18
  242.2 0.1 broadcast_compare_fusion
  242.2 2.7 copy.45
  245.0 2.3 fusion.7
  247.3 46.2 %pmax.7 = f32[8,16,2]{2,1,0:T(8,128)S(1)} all-reduce(f32[8,16,2]{2,1,0:T(8,128)S(1)} %get-tuple-element.22), channel_id=1, replica_groups=mesh['dp'=4,'tp'=16] {'tp'}, use_global_device_ids=true, to_apply=%region_1.2 | all-reduce | flops 256 | bytes 2048 | tf_op jit(solution)/shard_map/pmax | solution.py:30
  293.5 0.4 fusion.4
  293.9 2.7 copy.49
  296.7 1.3 convolution_multiply_fusion
  297.9 0.1 copy.51
  298.0 0.2 copy.50
  298.2 0.3 copy.52
  298.5 0.7 pad_maximum_fusion
  299.2 0.1 reduce-scatter.2.cloned.1.call-update
  299.2 6.9 %copy.54 = bf16[8,128,16,128]{3,2,1,0:T(8,128)(2,1)} copy(bf16[8,128,16,128]{3,0,1,2:T(8,128)(2,1)} %bitcast.22) | data formatting | bytes 8388608
  306.1 6.9 %copy.55 = bf16[8,128,16,128]{3,2,1,0:T(8,128)(2,1)} copy(bf16[8,128,16,128]{3,0,1,2:T(8,128)(2,1)} %bitcast.17) | data formatting | bytes 8388608
  313.0 39.2 %reduce-scatter.2.cloned.1.call-done = f32[8,2,129]{2,0,1:T(8,128)} async-done(((f32[8,32,129]{2,0,1:T(8,128)}), f32[8,2,129]{2,0,1:T(8,128)}) %reduce-scatter.2.cloned.1.call-update) | async-done | bytes 8272 | tf_op jit(solution)/shard_map/reduce_scatter | solution.py:34
  352.3 0.8 slice_reduce_fusion
  353.1 0.8 fusion.3
  353.9 0.6 copy.53
  (9 shorter events, 0.1 us)
Async XLA Ops:
  131.0 5.1 %copy-start = (bf16[8,2,128]{2,1,0:T(2,128)(2,1)S(1)}, bf16[8,2,128]{2,1,0:T(2,128)(2,1)}, u32[]{:S(2)}) copy-start(bf16[8,2,128]{2,1,0:T(2,128)(2,1)} %param.6) | copy-start | bytes 12292
  131.0 111.1 %copy-start.1 = (s32[8]{0:T(128)S(1)}, s32[8]{0:T(128)}, u32[]{:S(2)}) copy-start(s32[8]{0:T(128)} %param.11) | copy-start | bytes 100
  131.0 162.9 %all-to-all-start.1 = ((bf16[8,2048,1,128]{3,0,2,1:T(8,128)(2,1)}), bf16[8,2048,1,128]{3,0,2,1:T(8,128)(2,1)}, u32[]{:S(2)}, u32[]{:S(2)}) async-start(bf16[8,2048,1,128]{3,0,2,1:T(8,128)(2,1)} %get-tuple-element.20), calls=%async_computation.1 | async-start | bytes 8388608 | tf_op jit(solution)/shard_map/all_to_all | solution.py:17
  136.1 216.2 %reduce-scatter.2.cloned.1.call-start = ((), (), s32[]{:S(2)}) async-start(), calls=%async_computation.3 | async-start | bytes 278528 | tf_op jit(solution)/shard_map/reduce_scatter | solution.py:34
Sparse Core Ops, SparseCore 0:
  299.4 52.8 reduce-scatter.1
where the time goes:
time: 362 us; the launch traced here: 361 us
  blocking collectives  257 us (71%)
  waiting for transfers between devices  39.3 us (11%)
  local copies, waits for them, and re-layouts  21.2 us (6%)
  other arithmetic  21 us (6%)
  between operations  14.1 us (4%)
  starting transfers between devices  5.12 us (1%)
    all_gather x1, blocking collectives, local_step(): q_all = lax.all_gather(query, 'tp', axis=1, tiled=True)  106 us
    all_to_all x1, blocking collectives, local_step(): k_seq = lax.all_to_all(k_upd, 'tp', 1, 2, tiled=True)  105 us
    pmax x1, blocking collectives, local_step(): glob_max = lax.pmax(part_max, 'tp')  46.2 us
    reduce_scatter x1, waiting for transfers between devices, local_step(): own_heads = lax.psum_scatter(stacked, 'tp', scatter_dimension=1, tiled=True)  39.2 us
    select_n x1, other arithmetic, local_step(): v_upd = jnp.where(new_slot, v_new[:, None], v_cache)  18.2 us
    unnamed x8, local copies, waits for them, and re-layouts  14.4 us
  transfers between devices with their start and end apart: 2, of which 1 were waited for; matrix products, arithmetic and copies ran while one was open for 5% of the time, Pallas kernels for 0%

commit v1 on v0

v1 whole, which is shorter than its diff:
```python
import jax
import jax.numpy as jnp
from jax import lax
from jax.experimental import pallas as pl
from jax.experimental.pallas import tpu as pltpu
from jax.sharding import PartitionSpec as P

MASK_VALUE = -1e30
MESH = pl.DeviceIdType.MESH


def exchange_kernel(n, q_ref, k_hbm, v_hbm, kn_hbm, vn_hbm, kn_ref, vn_ref, lens_ref,
                    o_ref, rk, rv, rkn, rvn, kbuf, vbuf, load_sem, own_sem, send_sem, recv_sem):
    me = lax.axis_index("tp")
    batch, seq_len, head_dim = k_hbm.shape
    chunk = seq_len // n
    chips = n // 2
    chip, core = me // 2, me % 2

    loads = []
    for b in range(batch):
        for which, (src, dst) in enumerate(((k_hbm, kbuf), (v_hbm, vbuf))):
            loads.append(pltpu.make_async_copy(src.at[b], dst.at[b], load_sem.at[which, b]))
    for load in loads:
        load.start()

    barrier = pltpu.get_barrier_semaphore()
    for off in range(1, n):
        pl.semaphore_signal(barrier, inc=1, device_id={"tp": lax.rem(me + off, n)}, device_id_type=MESH)
    pl.semaphore_wait(barrier, n - 1)

    order = []
    for dist in range(chips // 2, 0, -1):
        steps = (dist,) if 2 * dist == chips else (dist, chips - dist)
        for step in steps:
            for other in (0, 1):
                order.append((step, other))
    order.append((0, 1))

    copies = []
    for step, other in order:
        peer = 2 * lax.rem(chip + step, chips) + lax.rem(core + other, 2)
        back = 2 * lax.rem(chip + chips - step, chips) + lax.rem(core + other, 2)
        window = pl.ds(pl.multiple_of(peer * chunk, chunk), chunk)
        for which, (src, dst) in enumerate(((kn_hbm, rkn), (vn_hbm, rvn))):
            copies.append((pltpu.make_async_remote_copy(
                src_ref=src, dst_ref=dst.at[me], send_sem=send_sem.at[2 + which, peer],
                recv_sem=recv_sem.at[2 + which, me], device_id={"tp": peer}, device_id_type=MESH),
                pltpu.make_async_copy(src, dst.at[back], recv_sem.at[2 + which, back])))
        for which, (src, dst) in enumerate(((k_hbm, rk), (v_hbm, rv))):
            copies.append((pltpu.make_async_remote_copy(
                src_ref=src.at[:, window], dst_ref=dst.at[me], send_sem=send_sem.at[which, peer],
                recv_sem=recv_sem.at[which, me], device_id={"tp": peer}, device_id_type=MESH),
                pltpu.make_async_copy(src.at[:, window], dst.at[back], recv_sem.at[which, back])))
    for copy, _ in copies:
        copy.start()

    for load in loads:
        load.wait()
    mine = pl.ds(pl.multiple_of(me * chunk, chunk), chunk)
    own = [pltpu.make_async_copy(kbuf.at[:, mine], rk.at[me], own_sem.at[0]),
           pltpu.make_async_copy(vbuf.at[:, mine], rv.at[me], own_sem.at[1]),
           pltpu.make_async_copy(kn_ref, rkn.at[me], own_sem.at[2]),
           pltpu.make_async_copy(vn_ref, rvn.at[me], own_sem.at[3])]
    for copy in own:
        copy.start()

    scale = head_dim ** -0.5

    def attend(b, carry):
        q = q_ref[b]
        length = lens_ref[b]
        row = lax.broadcasted_iota(jnp.int32, (batch, head_dim), 0) == b
        k_new = jnp.sum(jnp.where(row, kn_ref[...].astype(jnp.float32), 0.0), axis=0, keepdims=True)
        v_new = jnp.sum(jnp.where(row, vn_ref[...].astype(jnp.float32), 0.0), axis=0, keepdims=True)
        s = lax.dot_general(q, kbuf[b], (((1,), (1,)), ((), ())), preferred_element_type=jnp.float32)
        s_new = jnp.sum(q.astype(jnp.float32) * k_new, axis=1, keepdims=True)
        pos = lax.broadcasted_iota(jnp.int32, s.shape, 1)
        s = jnp.where(pos == length, s_new, s) * scale
        s = jnp.where(pos <= length, s, MASK_VALUE)
        e = jnp.exp(s - jnp.max(s, axis=1, keepdims=True))
        p = (e / jnp.sum(e, axis=1, keepdims=True)).astype(jnp.bfloat16).astype(jnp.float32)
        p_new = jnp.sum(jnp.where(pos == length, p, 0.0), axis=1, keepdims=True)
        p_old = jnp.where(pos == length, 0.0, p).astype(jnp.bfloat16)
        o = jnp.dot(p_old, vbuf[b], preferred_element_type=jnp.float32) + p_new * v_new
        o_ref[b] = o.astype(o_ref.dtype)
        return carry

    lax.fori_loop(0, batch, attend, 0)

    for copy in own:
        copy.wait()
    for copy, arrival in copies:
        copy.wait_send()
    for copy, arrival in copies:
        arrival.wait()


def solution(mesh):
    n = mesh.shape["tp"]

    def local_step(query, k_cache, v_cache, k_new, v_new, lens):
        batch, seq_len, _, head_dim = k_cache.shape
        chunk = seq_len // n
        k = k_cache.reshape(batch, seq_len, head_dim)
        v = v_cache.reshape(batch, seq_len, head_dim)
        kn = k_new.reshape(batch, head_dim)
        vn = v_new.reshape(batch, head_dim)
        anywhere = pl.BlockSpec(memory_space=pl.ANY)
        vmem = pl.BlockSpec(memory_space=pltpu.VMEM)
        dtype = k.dtype
        attn, rk, rv, rkn, rvn = pl.pallas_call(
            lambda *refs: exchange_kernel(n, *refs),
            name="exchange",
            out_shape=(jax.ShapeDtypeStruct(query.shape, query.dtype),
                       jax.ShapeDtypeStruct((n, batch, chunk, head_dim), dtype),
                       jax.ShapeDtypeStruct((n, batch, chunk, head_dim), dtype),
                       jax.ShapeDtypeStruct((n, batch, head_dim), dtype),
                       jax.ShapeDtypeStruct((n, batch, head_dim), dtype)),
            in_specs=[vmem, anywhere, anywhere, anywhere, anywhere, vmem, vmem,
                      pl.BlockSpec(memory_space=pltpu.SMEM)],
            out_specs=(vmem, anywhere, anywhere, anywhere, anywhere),
            scratch_shapes=[
                pltpu.VMEM((batch, seq_len, head_dim), dtype),
                pltpu.VMEM((batch, seq_len, head_dim), dtype),
                pltpu.SemaphoreType.DMA((2, batch)),
                pltpu.SemaphoreType.DMA((4,)),
                pltpu.SemaphoreType.DMA((4, n)),
                pltpu.SemaphoreType.DMA((4, n)),
            ],
            compiler_params=pltpu.CompilerParams(collective_id=0, has_side_effects=True),
        )(query, k, v, kn, vn, kn, vn, lens)

        pos = lax.axis_index("tp") * chunk + lax.broadcasted_iota(jnp.int32, (1, chunk, 1, 1), 1)
        new_slot = pos == lens[:, None, None, None]

        def finish(received, new):
            rows = jnp.transpose(received, (1, 2, 0, 3))
            return jnp.where(new_slot, jnp.transpose(new, (1, 0, 2))[:, None], rows)

        return attn, finish(rk, rkn), finish(rv, rvn)

    head_spec = P("dp", "tp")
    entry_spec = P("dp", None, "tp")
    return jax.shard_map(local_step, mesh=mesh, in_specs=(head_spec, entry_spec, entry_spec, head_spec, head_spec, P("dp")), out_specs=(head_spec, P("dp", "tp"), P("dp", "tp")), check_vma=False)
```

time: 362 us -> 212 us (0.59)
  blocking collectives: 257 us -> 0 us
  Pallas kernels: 0 us -> 195 us
  waiting for transfers between devices: 39.3 us -> 0 us
  other arithmetic: 21 us -> 4.72 us
  between operations: 14.1 us -> 0.66 us
  local copies, waits for them, and re-layouts: 21.2 us -> 10.3 us
  starting transfers between devices: 5.12 us -> 0 us
    pallas_call x0 -> x1, Pallas kernels: none -> 195 us  [local_step(): pl.pallas_call(lambda *refs: exchange_kernel(n, *refs), name='exchange',...]
    all_gather x1 -> x0, blocking collectives: 106 us -> none  [local_step(): q_all = lax.all_gather(query, 'tp', axis=1, tiled=True)]
    all_to_all x1 -> x0, blocking collectives: 105 us -> none  [local_step(): k_seq = lax.all_to_all(k_upd, 'tp', 1, 2, tiled=True)]
    pmax x1 -> x0, blocking collectives: 46.2 us -> none  [local_step(): glob_max = lax.pmax(part_max, 'tp')]
    reduce_scatter x1 -> x0, waiting for transfers between devices: 39.2 us -> none  [local_step(): own_heads = lax.psum_scatter(stacked, 'tp', scatter_dimension=1, tiled=True)]
    select_n x1, other arithmetic: 18.2 us -> 3.99 us  [finish(): return jnp.where(new_slot, jnp.transpose(new, (1, 0, 2))[:, None], rows)]
    all_to_all x2 -> x0, local copies, waits for them, and re-layouts: 5.46 us -> none  [the longest x1 2.73 us: local_step(): v_seq = lax.all_to_all(v_upd, 'tp', 1, 2, tiled=True)]
    all_to_all x1 -> x0, starting transfers between devices: 5.05 us -> none  [local_step(): v_seq = lax.all_to_all(v_upd, 'tp', 1, 2, tiled=True)]
  transfers between devices with their start and end apart: 2 -> 0, of which waited for: 1 -> 0; matrix products, arithmetic and copies ran while one was open for 5% -> 0% of each run, Pallas kernels for 0% -> 0%
where the time goes in v1:
time: 212 us; the launch traced here: 211 us
  Pallas kernels  195 us (92%)
  local copies, waits for them, and re-layouts  10.3 us (5%)
  other arithmetic  4.72 us (2%)
    pallas_call x1, Pallas kernels, local_step(): pl.pallas_call(lambda *refs: exchange_kernel(n, *refs), name='exchange',...  195 us
    unnamed x5, local copies, waits for them, and re-layouts  10.3 us

profile of v1, /device:TPU:22, one launch (start us, length us, event | category | flops | bytes accessed | tf_op | source)
XLA Modules:
  0.0 210.9 jit_solution(17165166457587347628)
XLA Ops:
  0.6 0.7 broadcast_compare_fusion
  1.4 195.2 %exchange.1 = (bf16[8,2,128]{2,1,0:T(2,128)(2,1)}, bf16[16,8,128,128]{3,2,1,0:T(8,128)(2,1)}, bf16[16,8,128,128]{3,2,1,0:T(8,128)(2,1)}, bf16[16,8,128]{2,1,0:T(8,128)(2,1)}, bf16[16,8,128]{2,1,0:T(8,128)(2,1)}) custom-call(bf16[8,2,128]{2,1,0:T(2,128)(2,1)} %refs_0_.1, bf16[8,2048,128]{2,1,0:T(8,128)(2,1)} %bitcast.10, bf16[8,2048,128]{2,1,0:T(8,128)(2,1)} %bitcast.11, ...), custom_call_target="tpu_custom_call" | custom-call | tf_op jit(solution)/shard_map/exchange/pallas_call | solution.py:112
  196.6 4.0 %bitcast_select_fusion = (bf16[8,128,16,128]{3,1,0,2:T(8,128)(2,1)S(1)}, bf16[8,128,16,128]{3,1,0,2:T(8,128)(2,1)S(1)}) fusion(bf16[16,8,128,128]{3,2,1,0:T(8,128)(2,1)} %get-tuple-element.12, pred[8,128]{1,0:T(8,128)(4,1)S(1)} %broadcast_compare_fusion, bf16[8,16,128]{2,0,1:T(8,128)(2,1)} %bitcast.13, bf16[16,8,128,128]{3,2,1,0:T(8,128)(2,1)} %get-tuple-element.10, ...), kind=kLoop, calls=%fused_computation | loop fusion | flops 4194304 | bytes 16843776 | tf_op jit(solution)/shard_map/jit(_where)/select_n | solution.py:139
  200.6 4.9 %copy.10 = bf16[8,128,16,128]{3,2,1,0:T(8,128)(2,1)} copy(bf16[8,128,16,128]{3,1,0,2:T(8,128)(2,1)S(1)} %get-tuple-element.16) | data formatting | bytes 8388608
  205.5 0.0 copy-start
  205.5 4.9 %copy.9 = bf16[8,128,16,128]{3,2,1,0:T(8,128)(2,1)} copy(bf16[8,128,16,128]{3,1,0,2:T(8,128)(2,1)S(1)} %get-tuple-element.17) | data formatting | bytes 8388608
  210.3 0.0 copy-done
  210.3 0.6 copy.12
  (1 shorter events, 0.0 us)
Async XLA Ops:
  205.5 4.9 %copy-start = (bf16[8,2,128]{2,1,0:T(2,128)(2,1)S(1)}, bf16[8,2,128]{2,1,0:T(2,128)(2,1)}, u32[]{:S(2)}) copy-start(bf16[8,2,128]{2,1,0:T(2,128)(2,1)} %get-tuple-element.21) | copy-start | bytes 12292
